TPU v7x, 32 devices: a whole 2x2x4 slice. The times are simulated.
32 devices in a mesh: dp: 4 (over y, x), fsdp: 8 (over z, core).
Axes of the slice: x: 2, y: 2, z: 4, core: 2. Of those that a mesh axis runs over, the one named last changes fastest.
Arguments:
- grads: bfloat16 [4, 16, 512, 512], P('dp', None, 'fsdp'), may hold values from -4 to 4
- left_stats: float32 [8, 4, 512, 512], P('fsdp', None, 'dp'), may hold values from -0.5 to 9, as said below
- right_stats: float32 [8, 4, 512, 512], P('fsdp', None, 'dp'), may hold values from -0.5 to 9, as said below
- left_root: bfloat16 [8, 4, 512, 512], P('fsdp', None, 'dp'), may hold values from -0.5 to 14, as said below
- right_root: bfloat16 [8, 4, 512, 512], P('fsdp'), may hold values from -0.5 to 14, as said below
- second_moment: float32 [8, 4, 512, 512], P('fsdp', None, 'dp'), may hold values from 0.2 to 2
- slot_block: int32 [8, 4], replicated, may hold values from 0 to 15, as said below
- counts: int32 [8], replicated, may hold values from 0 to 4, as said below
Outputs:
- left_new: float32 [8, 4, 512, 512], P('fsdp', None, 'dp')
- right_new: float32 [8, 4, 512, 512], P('fsdp', None, 'dp')
- second_new: float32 [8, 4, 512, 512], P('fsdp', None, 'dp')
- update: float32 [8, 4, 512, 512], P('fsdp', None, 'dp')
Inputs may be any that keep to these rules, and one draw needn't show every extreme that they name: Every owner holds counts[o] blocks; the counts sum to 16, and some owner holds exactly 4. `slot_block`: the first counts[o] slots of owner o name distinct blocks, every block is named by exactly one such slot, and later slots name arbitrary blocks. `left_stats`: Symmetric. `right_stats`: Symmetric. `left_root`: Symmetric. `right_root`: Symmetric.
All inputs are finite; a program needn't handle non-finite values.
Results may differ from a plain program's by a relative error of at most 0.015.
Values may be sent and summed in bfloat16 or wider, within the bound.
No kernel may reach another device: no remote copies, remote signals or barrier semaphores. Data moves between devices by JAX's collectives and lax.ppermute only.
A program may use at most 64 MiB of HBM per device.

v0:
```python
import functools

import jax
import jax.numpy as jnp
from jax import lax
from jax.experimental import pallas as pl
from jax.experimental.pallas import tpu as pltpu
from jax.sharding import PartitionSpec as P


SHAMPOO_BETA = 0.998
ADAM_BETA = 0.95
EPSILON = 1e-08
SMALL = 8 * 1024 * 1024
SMEM = pltpu.SMEM
VMEM = pltpu.VMEM


def exchange(value, axis, distance):
    size = lax.axis_size(axis)
    return lax.ppermute(value, axis, [(i, i ^ distance) for i in range(size)])


def in_hbm(value):
    return pltpu.with_memory_space_constraint(value, pltpu.HBM)


def in_vmem(value):
    return pltpu.with_memory_space_constraint(value, pltpu.VMEM)


def in_smem(value):
    return pltpu.with_memory_space_constraint(value, pltpu.SMEM)


def call(kernel, out, ins, in_specs, out_specs, scratch=(), **more):
    return pl.pallas_call(
        kernel,
        out_shape=out,
        in_specs=in_specs,
        out_specs=out_specs,
        scratch_shapes=list(scratch),
        compiler_params=pltpu.CompilerParams(vmem_limit_bytes=SMALL),
        cost_estimate=pl.CostEstimate(flops=10_000_000, bytes_accessed=1_000_000, transcendentals=0),
        **more,
    )(*ins)


IN_SMEM = pl.BlockSpec(memory_space=SMEM)
IN_VMEM = pl.BlockSpec(memory_space=VMEM)
IN_HBM = pl.BlockSpec(memory_space=pltpu.HBM)


def first_place(counts, owner):
    start = jnp.int32(0)
    for at in range(counts.shape[0]):
        start = start + jnp.where(at < owner, counts[at], 0)
    return start


def send_blocks(part, chunks, order, grads, outs, sems):
    ways, group, rows = len(outs), outs[0].shape[0], grads.shape[1] // chunks
    me = lax.axis_index("dp")
    copies = []
    for distance in list(range(1, ways)) + [0]:
        for at in range(group):
            block = order[at * ways + (me ^ distance)]
            sem = sems.at[distance * group + at]
            copy = pltpu.make_async_copy(grads.at[block, pl.ds(part * rows, rows)], outs[distance].at[at], sem)
            copy.start()
            copies.append(copy)
    return copies


def deal_kernel(chunks, slot_block, counts, grads, *rest):
    outs, (order, meta, picks, sems) = rest[:-4], rest[-4:]
    ways = len(outs)
    cap, owners = slot_block.shape
    place = jnp.int32(0)
    for owner in range(owners):
        for slot in range(cap):

            @pl.when(slot < counts[owner])
            def _():
                order[place + slot] = slot_block[slot, owner]

        place = place + counts[owner]
    copies = send_blocks(0, chunks, order, grads, outs, sems)
    me, owner_here = lax.axis_index("dp"), lax.axis_index("fsdp")
    start = first_place(counts, owner_here)
    for distance in range(ways):
        meta[distance] = ((me ^ distance) - start + owners * ways * 2) % ways
    meta[ways] = counts[owner_here]
    for distance in range(owners):
        owner = owner_here ^ distance
        start = first_place(counts, owner)
        slot = (me - start + owners * ways * 2) % ways
        picks[distance] = jnp.where(slot < counts[owner], (start + slot) // ways, 0)
    for copy in copies:
        copy.wait()


def deal(slot_block, counts, grads, ways, chunks):
    blocks, rows, width = grads.shape
    sizes = (blocks, ways + 1, counts.shape[0])
    *outs, order, meta, picks = call(
        functools.partial(deal_kernel, chunks),
        (pltpu.VMEM((blocks // ways, rows // chunks, width), grads.dtype),) * ways
        + tuple(pltpu.SMEM((size,), jnp.int32) for size in sizes),
        (in_hbm(slot_block.T), in_hbm(counts), in_hbm(grads)),
        [IN_SMEM, IN_SMEM, IN_HBM],
        (IN_VMEM,) * ways + (IN_SMEM,) * 3,
        [pltpu.SemaphoreType.DMA((blocks,))],
    )
    return outs, order, meta, picks


def more_kernel(part, chunks, order, meta, grads, root, moment, *rest):
    outs, (lent, wide, sems, more) = rest[:-4], rest[-4:]
    copies = send_blocks(part, chunks, order, grads, outs, sems)
    slot = meta[len(outs) - 1]
    far = pltpu.make_async_copy(moment.at[slot], wide, more.at[0])
    near = pltpu.make_async_copy(root.at[slot], lent.at[0], more.at[1])
    far.start()
    near.start()
    far.wait()
    lent[1] = wide[...].astype(lent.dtype)
    for copy in (near, *copies):
        copy.wait()


def deal_more(order, meta, grads, root, moment, ways, part, chunks):
    blocks, rows, width = grads.shape
    _, high, wide = root.shape
    return call(
        functools.partial(more_kernel, part, chunks),
        (pltpu.VMEM((blocks // ways, rows // chunks, width), grads.dtype),) * ways
        + (pltpu.VMEM((2, high, wide), jnp.bfloat16),),
        (in_smem(order), in_smem(meta), in_hbm(grads), in_hbm(root), in_hbm(moment)),
        [IN_SMEM, IN_SMEM] + [IN_HBM] * 3,
        (IN_VMEM,) * (ways + 1),
        [VMEM((high, wide), jnp.float32), pltpu.SemaphoreType.DMA((blocks,)), pltpu.SemaphoreType.DMA((2,))],
    )


def fetch_kernel(*refs):
    count = len(refs) // 2
    sources, outs, sems = refs[:count], refs[count:-1], refs[-1]
    copies = [pltpu.make_async_copy(a, b, sems.at[at]) for at, (a, b) in enumerate(zip(sources, outs))]
    for copy in copies:
        copy.start()
    for copy in copies:
        copy.wait()


def fetch(arrays):
    return call(
        fetch_kernel,
        tuple(pltpu.VMEM(x.shape, x.dtype) for x in arrays),
        [in_hbm(x) for x in arrays],
        [IN_HBM] * len(arrays),
        (IN_VMEM,) * len(arrays),
        [pltpu.SemaphoreType.DMA((len(arrays),))],
    )


def add_parts(parts, held):
    total = parts[0][...].astype(jnp.float32)
    for part in parts[1:]:
        total = total + part[...].astype(jnp.float32)
    held[...] = total.astype(held.dtype)


def sort_kernel(picks, *rest):
    parts, (same, other, held) = rest[:-3], rest[-3:]
    add_parts(parts, held)
    for distance in range(same.shape[0]):
        same[distance] = held[picks[2 * distance]]
        other[distance] = held[picks[2 * distance + 1]]


def sort(picks, parts, owners):
    group = parts[0].shape
    half = pltpu.VMEM((owners // 2,) + group[1:], parts[0].dtype)
    return call(
        sort_kernel,
        (half, half),
        (in_smem(picks), *[in_vmem(x) for x in parts]),
        [IN_SMEM] + [IN_VMEM] * len(parts),
        (IN_VMEM, IN_VMEM),
        [VMEM(group, parts[0].dtype)],
    )


def pair_kernel(same, other, *outs):
    for at, out in enumerate(outs):
        out[0] = same[at + 1]
        out[1] = other[at + 1]


def pair(same, other):
    out = pltpu.VMEM((2,) + same.shape[1:], same.dtype)
    count = same.shape[0] - 1
    return call(pair_kernel, (out,) * count, (in_vmem(same), in_vmem(other)), [IN_VMEM] * 2, (IN_VMEM,) * count)


def land_kernel(same, other, *rest):
    got, out = rest[:-1], rest[-1]
    me = lax.axis_index("fsdp")
    out[me] = same[0]
    out[me ^ 1] = other[0]
    for at, pieces in enumerate(got):
        out[me ^ (2 * at + 2)] = pieces[0]
        out[me ^ (2 * at + 3)] = pieces[1]


def land(same, other, got):
    out = pltpu.VMEM((2 * same.shape[0],) + same.shape[1:], same.dtype)
    ins = [in_vmem(x) for x in (same, other, *got)]
    return call(land_kernel, out, ins, [IN_VMEM] * len(ins), IN_VMEM)


def assemble(whole, pieces):
    slabs, rows, _ = pieces[0].shape
    for slab in range(slabs):
        for part, piece in enumerate(pieces):
            at = (slab * len(pieces) + part) * rows
            whole[at : at + rows, :] = piece[slab]


def precondition(root, whole, right):
    half = jnp.dot(root, whole[...], preferred_element_type=jnp.float32).astype(jnp.bfloat16)
    return jnp.dot(half, right, preferred_element_type=jnp.float32)


def own_rows(device, rows):
    return pl.ds(pl.multiple_of(device * rows, rows), rows)


def second_of(live, old, values):
    return jnp.where(live, ADAM_BETA * old + (1.0 - ADAM_BETA) * values * values, old)


def norms_of(precond, values, moment):
    adam = values / (jnp.sqrt(moment) + EPSILON)
    return jnp.sum(precond * precond), jnp.sum(adam * adam)


def put_norms(kept, slot, sums):
    row = lax.broadcasted_iota(jnp.int32, kept.shape, 0)
    return jnp.where(row == 2 * slot, sums[0], jnp.where(row == 2 * slot + 1, sums[1], kept))


class Writes:
    def __init__(self, stage, sems):
        self.stage, self.sems, self.copies = stage, sems, []

    def put(self, value, out, slot):
        at = len(self.copies)
        self.stage[at] = value
        self.copies.append(pltpu.make_async_copy(self.stage.at[at], out.at[slot], self.sems.at[at]))
        self.copies[-1].start()

    def wait(self):
        for copy in self.copies:
            copy.wait()


def work_direct(slot, live, whole, root, right, moment, precond_out, moment_out, writes):
    precond = precondition(root[slot], whole, right[slot])
    if precond_out is not None:
        precond_out[slot] = precond
    values = whole[own_rows(lax.axis_index("dp"), root.shape[1]), :].astype(jnp.float32)
    new = second_of(live, moment[slot], values)
    writes.put(new, moment_out, slot)
    return precond, values, new


def work_gram(slot, live, whole, left, right, left_out, right_out, writes):
    rows = own_rows(lax.axis_index("dp"), left.shape[1])
    for part, dims, old, out in (
        (whole[rows, :], ((1,), (1,)), left, left_out),
        (whole[:, rows], ((0,), (0,)), right, right_out),
    ):
        term = lax.dot_general(part, whole[...], (dims, ((), ())), preferred_element_type=jnp.float32)
        kept = old[slot]
        writes.put(jnp.where(live, SHAMPOO_BETA * kept + (1.0 - SHAMPOO_BETA) * term, kept), out, slot)


def own_kernel(ways, meta, a, b, root, right, moment, left, right_stats, lent, *rest):
    precond_out, moment_out, norms, left_out, right_out, whole, stage, sems = rest
    writes = Writes(stage, sems)
    assemble(whole, (a, b))
    slot, held = meta[0], meta[ways]
    live = slot < held
    sums = norms_of(*work_direct(slot, live, whole, root, right, moment, precond_out, moment_out, writes))
    values = whole[own_rows(lax.axis_index("dp") ^ (ways - 1), root.shape[1]), :].astype(jnp.float32)
    there = precondition(lent[0], whole, right[slot])
    more = norms_of(there, values, second_of(live, lent[1].astype(jnp.float32), values))
    norms[...] = put_norms(jnp.zeros(norms.shape, jnp.float32), slot, (sums[0] + more[0], sums[1] + more[1]))
    work_gram(slot, live, whole, left, right_stats, left_out, right_out, writes)
    writes.wait()


def visit_kernel(distances, grams, ways, meta, *rest):
    rest = list(rest)
    take = lambda n: [rest.pop(0) for _ in range(n)]
    pieces = [take(2) for _ in distances]
    root, right, moment = take(3)
    stats = take(2) if grams else None
    take(2)
    (norms_in,) = take(1)
    take(2 if grams else 0)
    precond_out, moment_out, norms = take(3)
    stats_out = take(2) if grams else None
    whole, stage, sems = rest
    writes = Writes(stage, sems)
    total = norms_in[...]
    for at, distance in enumerate(distances):
        here = whole.at[at]
        assemble(here, pieces[at])
        slot = meta[distance]
        live = slot < meta[ways]
        got = work_direct(slot, live, here, root, right, moment, precond_out, moment_out, writes)
        total = put_norms(total, slot, norms_of(*got))
        if grams:
            work_gram(slot, live, here, *stats, *stats_out, writes)
    norms[...] = total
    writes.wait()


def gram_kernel(distances, ways, meta, *rest):
    pieces, rest = rest[: 2 * len(distances)], rest[2 * len(distances) :]
    left, right_stats, _, _, left_out, right_out, whole, stage, sems = rest
    writes = Writes(stage, sems)
    for at, distance in enumerate(distances):
        assemble(whole.at[at], pieces[2 * at : 2 * at + 2])
        slot = meta[distance]
        work_gram(slot, slot < meta[ways], whole.at[at], left, right_stats, left_out, right_out, writes)
    writes.wait()


def last_kernel(ways, meta, a, b, root, right, moment, left, right_stats, precond, *rest):
    norms, rest = rest[:ways], rest[ways + 3 :]
    update, moment_out, left_out, right_out, whole, stage, sems = rest
    writes = Writes(stage, sems)
    total = norms[0][...]
    for part in norms[1:]:
        total = total + part[...]
    row = lax.broadcasted_iota(jnp.int32, total.shape, 0)

    def scaled(value, slot):
        live = slot < meta[ways]
        pick = lambda at: jnp.sum(jnp.where(row == at, total, 0.0), axis=0, keepdims=True)[:, 0:1]
        scale = jnp.where(live, jnp.sqrt(pick(2 * slot + 1) / jnp.where(live, pick(2 * slot), 1.0)), 0.0)
        return jnp.where(live, value * scale, 0.0)

    for distance in range(ways - 1):
        slot = meta[distance]
        writes.put(scaled(precond[slot], slot), update, slot)
    assemble(whole, (a, b))
    slot = meta[ways - 1]
    live = slot < meta[ways]
    value, _, _ = work_direct(slot, live, whole, root, right, moment, None, moment_out, writes)
    writes.put(scaled(value, slot), update, slot)
    work_gram(slot, live, whole, left, right_stats, left_out, right_out, writes)
    writes.wait()


def work(kernel, ways, meta, ins, kept, outs, staged, wholes):
    width = ins[0].shape[-1]
    rows = outs[0].shape[1]
    args = [in_smem(meta)] + [in_vmem(x) for x in ins]
    specs = [IN_SMEM] + [IN_VMEM] * len(ins)
    alias = {}
    for array, near, out in kept:
        if out is not None:
            alias[len(args)] = out
        args.append(in_vmem(array) if near else in_hbm(array))
        specs.append(IN_VMEM if near else IN_HBM)
    spec_of = lambda ref: IN_HBM if ref.memory_space == pltpu.HBM else IN_VMEM
    return call(
        functools.partial(kernel, ways),
        tuple(outs),
        args,
        specs,
        tuple(spec_of(x) for x in outs),
        [
            VMEM(wholes + (width, width), jnp.bfloat16),
            VMEM((staged, rows, width), jnp.float32),
            pltpu.SemaphoreType.DMA((staged,)),
        ],
        input_output_aliases=alias,
    )


def on_device_direct(
    grads, left_stats, right_stats, left_root, right_root, second_moment, slot_block, counts
):
    ways, chunks = lax.axis_size("dp"), 2
    owners, slots = slot_block.shape
    first = (left_root[0], right_root[0], second_moment[0])
    second = (left_stats[0], right_stats[0])
    parts = []
    for part in range(chunks):
        if part == 0:
            dealt, order, meta, picks = deal(slot_block, counts, grads[0], ways, chunks)
        else:
            *dealt, lent = deal_more(
                order, meta, grads[0], left_root[0], second_moment[0], ways, part, chunks
            )
        parts.append(list(dealt[:1]))
        for k in range(1, ways):
            parts[part].append(exchange(dealt[k], "dp", k))
    lent = exchange(lent, "dp", ways - 1)
    first = fetch(first)
    second = fetch(second)
    blocks = []
    for part in range(chunks):
        same, other = sort(picks, parts[part], owners)
        other = exchange(other, "fsdp", 1)
        sent = pair(same, other)
        got = [None] * len(sent)
        for k in range(len(sent)):
            got[k] = exchange(sent[k], "fsdp", 2 * k + 2)
        blocks.append(land(same, other, got))
    side, over = [], []
    for part in range(chunks):
        side.append(exchange(blocks[part], "dp", 1))
        over.append(exchange(blocks[part], "dp", 2))
    relay0 = exchange(side[0], "dp", 2)
    relay1 = exchange(over[1], "dp", 1)

    state = (slots,) + left_stats.shape[2:]
    near, far = pltpu.VMEM(state, jnp.float32), pltpu.HBM(state, jnp.float32)
    norm = pltpu.VMEM((-(-2 * slots // 8) * 8, 128), jnp.float32)
    ins = (*blocks, *first, *second, lent)
    precond, moment, norms, left, right = work(own_kernel, ways, meta, ins, (), (near, far, norm, far, far), 4, ())
    kernel = functools.partial(visit_kernel, (1,), True)
    kept = ((precond, True, 0), (moment, False, 1), (norms, True, None), (left, False, 3), (right, False, 4))
    outs = (near, far, norm, far, far)
    ins = (*side, *first, *second)
    precond, moment, norms, left, right = work(kernel, ways, meta, ins, kept, outs, 3, (1,))
    kernel = functools.partial(visit_kernel, (2,), False)
    kept = ((precond, True, 0), (moment, False, 1), (norms, True, None))
    ins = (*over, *first)
    precond, moment, norms = work(kernel, ways, meta, ins, kept, (near, far, norm), 1, (1,))
    all_norms = [norms]
    for k in range(1, ways):
        all_norms.append(exchange(norms, "dp", k))
    kept = ((left, False, 0), (right, False, 1))
    kernel = functools.partial(gram_kernel, (2,))
    left, right = work(kernel, ways, meta, (*over, *second), kept, (far, far), 2, (1,))
    ins = (relay0, relay1, *first, *second, precond, *all_norms)
    kept = ((moment, False, 1), (left, False, 2), (right, False, 3))
    update, second_new, left_new, right_new = work(last_kernel, ways, meta, ins, kept, (far,) * 4, ways + 3, ())
    return (left_new[None], right_new[None], second_new[None], update[None])


def on_device(
    grads, left_stats, right_stats, left_root, right_root, second_moment, slot_block, counts
):
    slot_count = slot_block.shape[1]
    owner_count = slot_block.shape[0]
    block_order = left_root.shape[3]
    partial_value = grads[0]
    block_count = partial_value.shape[0]
    slab_rows = partial_value.shape[1]
    flat_slots = slot_block.reshape(-1)
    live_slots = (jnp.arange(slot_count, dtype=jnp.int32)[None, :] < counts[:, None]).reshape(-1)
    flat_partial = partial_value.reshape(block_count, slab_rows * block_order).astype(jnp.float32)
    summed = lax.psum_scatter(
        flat_partial.astype(jnp.bfloat16), "dp", scatter_dimension=1, tiled=True
    )
    picked = jnp.where(live_slots[:, None], summed[flat_slots], jnp.zeros((), jnp.bfloat16))
    received = lax.all_to_all(picked, "fsdp", split_axis=0, concat_axis=1, tiled=True)
    piece_width = summed.shape[1]
    received = received.reshape(slot_count, owner_count, piece_width)
    gathered = lax.all_gather(received, "dp", axis=2, tiled=True)
    grad_full = gathered.reshape(slot_count, block_order, block_order)
    slab_width = block_order // lax.axis_size("dp")
    row_start = lax.axis_index("dp") * slab_width
    row_grad = lax.dynamic_slice_in_dim(grad_full, row_start, slab_width, 1)
    column_grad = lax.dynamic_slice_in_dim(grad_full, row_start, slab_width, 2)
    owned_here = jnp.arange(slot_count, dtype=jnp.int32) < counts[lax.axis_index("fsdp")]
    keep_mask = owned_here[:, None, None]
    left_term = jnp.einsum("crk,cjk->crj", row_grad, grad_full, preferred_element_type=jnp.float32)
    right_term = jnp.einsum(
        "ckr,ckj->crj", column_grad, grad_full, preferred_element_type=jnp.float32
    )
    left_old = left_stats[0]
    right_old = right_stats[0]
    left_new = jnp.where(
        keep_mask, SHAMPOO_BETA * left_old + (1.0 - SHAMPOO_BETA) * left_term, left_old
    )
    right_new = jnp.where(
        keep_mask, SHAMPOO_BETA * right_old + (1.0 - SHAMPOO_BETA) * right_term, right_old
    )
    left_half = jnp.einsum(
        "crk,ckj->crj", left_root[0], grad_full, preferred_element_type=jnp.float32
    ).astype(jnp.bfloat16)
    precond = jnp.einsum(
        "crk,ckj->crj", left_half, right_root[0], preferred_element_type=jnp.float32
    )
    row_values = row_grad.astype(jnp.float32)
    moment_old = second_moment[0]
    second_new = jnp.where(
        keep_mask, ADAM_BETA * moment_old + (1.0 - ADAM_BETA) * row_values * row_values, moment_old
    )
    adam = row_values / (jnp.sqrt(second_new) + EPSILON)
    precond_sum, adam_sum = lax.psum(
        (jnp.sum(precond * precond, axis=(1, 2)), jnp.sum(adam * adam, axis=(1, 2))), "dp"
    )
    graft_scale = jnp.where(
        owned_here, jnp.sqrt(adam_sum / jnp.where(owned_here, precond_sum, 1.0)), 0.0
    )
    update = precond * graft_scale[:, None, None]
    return (left_new[None], right_new[None], second_new[None], update[None])


def solution(mesh):
    in_specs = (
        P("dp", None, "fsdp", None),
        P("fsdp", None, "dp", None),
        P("fsdp", None, "dp", None),
        P("fsdp", None, "dp", None),
        P("fsdp", None, None, None),
        P("fsdp", None, "dp", None),
        P(),
        P(),
    )
    out_specs = (
        P("fsdp", None, "dp", None),
        P("fsdp", None, "dp", None),
        P("fsdp", None, "dp", None),
        P("fsdp", None, "dp", None),
    )

    ways, owners = mesh.shape["dp"], mesh.shape["fsdp"]
    square = ways == 4 and owners % 2 == 0 and owners & (owners - 1) == 0

    def fits(args):
        return square and args[6].shape[1] == ways and args[0].shape[1] % ways == 0

    def body(*args):
        return (on_device_direct if fits(args) else on_device)(*args)

    return jax.shard_map(body, mesh=mesh, in_specs=in_specs, out_specs=out_specs, check_vma=False)
```

profile of v0, /device:TPU:0, one launch (start us, length us, event | category | flops | bytes accessed | tf_op | source)
XLA Modules:
  0.0 69.0 jit_solution(5852587044628645060)
XLA Ops:
  0.6 2.0 %shard_map.111 = (bf16[4,32,512]{2,1,0:T(8,128)(2,1)S(1)}, bf16[4,32,512]{2,1,0:T(8,128)(2,1)S(1)}, bf16[4,32,512]{2,1,0:T(8,128)(2,1)S(1)}, bf16[4,32,512]{2,1,...) custom-call(s32[4,8]{1,0:T(4,128)} %bitcast.23, s32[8]{0:T(128)} %counts.1, ...), custom_call_target="tpu_custom_call" | custom-call | flops 10000000 | bytes 1000000 | tf_op jit(solution)/shard_map/pallas_call | solution.py:37
  2.7 1.5 %shard_map.115 = (bf16[4,32,512]{2,1,0:T(8,128)(2,1)S(1)}, bf16[4,32,512]{2,1,0:T(8,128)(2,1)S(1)}, bf16[4,32,512]{2,1,0:T(8,128)(2,1)S(1)}, bf16[4,32,512]{2,1,0:T(8,128)(2,1)S(1)}, bf16[2,128,512]{2,1,0:T(8,128)(2,1)S(1)}) custom-call(s32[16]{0:T(128)S(4)} %get-tuple-element.61.order, s32[5]{0:T(128)S(4)} %get-tuple-element.50.meta, ...), custom_call_target="tpu_custom_call" | custom-call | flops 10000000 | bytes 1000000 | tf_op jit(solution)/shard_map/pallas_call | solution.py:37
  4.1 3.1 %collective-permute-start.10 = (bf16[4,32,512]{2,1,0:T(8,128)(2,1)S(1)}, bf16[4,32,512]{2,1,0:T(8,128)(2,1)S(1)}, u32[]{:S(2)}, u32[]{:S(2)}) collective-permute-start(bf16[4,32,512]{2,1,0:T(8,128)(2,1)S(1)} %get-tuple-element.64), channel_id=1, source_target_pairs={{0,16},{8,24},{16,0},{24,8},{1,17},{9,25},{17,1},{25,9},{2,18},{10... | collective-permute-start | bytes 393224 | tf_op jit(solution)/shard_map/ppermute | solution.py:21
  7.2 1.4 %collective-permute-start.11 = (bf16[4,32,512]{2,1,0:T(8,128)(2,1)S(1)}, bf16[4,32,512]{2,1,0:T(8,128)(2,1)S(1)}, u32[]{:S(2)}, u32[]{:S(2)}) collective-permute-start(bf16[4,32,512]{2,1,0:T(8,128)(2,1)S(1)} %get-tuple-element.65), channel_id=1, source_target_pairs={{0,24},{8,16},{16,8},{24,0},{1,25},{9,17},{17,9},{25,1},{2,26},{10... | collective-permute-start | bytes 393224 | tf_op jit(solution)/shard_map/ppermute | solution.py:21
  8.7 1.9 %collective-permute-start = (bf16[4,32,512]{2,1,0:T(8,128)(2,1)S(1)}, bf16[4,32,512]{2,1,0:T(8,128)(2,1)S(1)}, u32[]{:S(2)}, u32[]{:S(2)}) collective-permute-start(bf16[4,32,512]{2,1,0:T(8,128)(2,1)S(1)} %get-tuple-element.53), channel_id=1, source_target_pairs={{0,8},{8,0},{16,24},{24,16},{1,9},{9,1},{17,25},{25,17},{2,10},{10... | collective-permute-start | bytes 393224 | tf_op jit(solution)/shard_map/ppermute | solution.py:21
  10.7 1.5 %collective-permute-start.1 = (bf16[4,32,512]{2,1,0:T(8,128)(2,1)S(1)}, bf16[4,32,512]{2,1,0:T(8,128)(2,1)S(1)}, u32[]{:S(2)}, u32[]{:S(2)}) collective-permute-start(bf16[4,32,512]{2,1,0:T(8,128)(2,1)S(1)} %get-tuple-element.54), channel_id=1, source_target_pairs={{0,16},{8,24},{16,0},{24,8},{1,17},{9,25},{17,1},{25,9},{2,18},{10... | collective-permute-start | bytes 393224 | tf_op jit(solution)/shard_map/ppermute | solution.py:21
  12.2 1.7 %collective-permute-done.10.rest_2_ = bf16[4,32,512]{2,1,0:T(8,128)(2,1)S(1)} collective-permute-done((bf16[4,32,512]{2,1,0:T(8,128)(2,1)S(1)}, bf16[4,32,512]{2,1,0:T(8,128)(2,1)S(1)}, u32[]{:S(2)}, u32[]{:S(2)}) %collective-permute-start.10) | collective-permute-done | bytes 131104 | tf_op jit(solution)/shard_map/ppermute | solution.py:21
  13.8 3.5 %collective-permute-start.2 = (bf16[4,32,512]{2,1,0:T(8,128)(2,1)S(1)}, bf16[4,32,512]{2,1,0:T(8,128)(2,1)S(1)}, u32[]{:S(2)}, u32[]{:S(2)}) collective-permute-start(bf16[4,32,512]{2,1,0:T(8,128)(2,1)S(1)} %get-tuple-element.55), channel_id=1, source_target_pairs={{0,24},{8,16},{16,8},{24,0},{1,25},{9,17},{17,9},{25,1},{2,26},{10... | collective-permute-start | bytes 393224 | tf_op jit(solution)/shard_map/ppermute | solution.py:21
  17.5 1.2 %collective-permute-done.rest_1_ = bf16[4,32,512]{2,1,0:T(8,128)(2,1)S(1)} collective-permute-done((bf16[4,32,512]{2,1,0:T(8,128)(2,1)S(1)}, bf16[4,32,512]{2,1,0:T(8,128)(2,1)S(1)}, u32[]{:S(2)}, u32[]{:S(2)}) %collective-permute-start) | collective-permute-done | bytes 131104 | tf_op jit(solution)/shard_map/ppermute | solution.py:21
  18.7 2.8 %collective-permute-done.2.rest_3_ = bf16[4,32,512]{2,1,0:T(8,128)(2,1)S(1)} collective-permute-done((bf16[4,32,512]{2,1,0:T(8,128)(2,1)S(1)}, bf16[4,32,512]{2,1,0:T(8,128)(2,1)S(1)}, u32[]{:S(2)}, u32[]{:S(2)}) %collective-permute-start.2) | collective-permute-done | bytes 131104 | tf_op jit(solution)/shard_map/ppermute | solution.py:21
  21.8 1.6 %collective-permute-start.13 = (bf16[2,32,512]{2,1,0:T(8,128)(2,1)S(1)}, bf16[2,32,512]{2,1,0:T(8,128)(2,1)S(1)}, u32[]{:S(2)}, u32[]{:S(2)}) collective-permute-start(bf16[2,32,512]{2,1,0:T(8,128)(2,1)S(1)} %get-tuple-element.68), channel_id=1, source_target_pairs={{0,2},{1,3},{2,0},{3,1},{4,6},{5,7},{6,4},{7,5},{8,10},{9,11},{10,... | collective-permute-start | bytes 196616 | tf_op jit(solution)/shard_map/ppermute | solution.py:21
  23.4 2.6 %collective-permute-start.14 = (bf16[2,32,512]{2,1,0:T(8,128)(2,1)S(1)}, bf16[2,32,512]{2,1,0:T(8,128)(2,1)S(1)}, u32[]{:S(2)}, u32[]{:S(2)}) collective-permute-start(bf16[2,32,512]{2,1,0:T(8,128)(2,1)S(1)} %get-tuple-element.69), channel_id=1, source_target_pairs={{0,4},{1,5},{2,6},{3,7},{4,0},{5,1},{6,2},{7,3},{8,12},{9,13},{10,... | collective-permute-start | bytes 196616 | tf_op jit(solution)/shard_map/ppermute | solution.py:21
  26.2 0.7 %collective-permute-start.4 = (bf16[2,32,512]{2,1,0:T(8,128)(2,1)S(1)}, bf16[2,32,512]{2,1,0:T(8,128)(2,1)S(1)}, u32[]{:S(2)}, u32[]{:S(2)}) collective-permute-start(bf16[2,32,512]{2,1,0:T(8,128)(2,1)S(1)} %get-tuple-element.58), channel_id=1, source_target_pairs={{0,2},{1,3},{2,0},{3,1},{4,6},{5,7},{6,4},{7,5},{8,10},{9,11},{10,... | collective-permute-start | bytes 196616 | tf_op jit(solution)/shard_map/ppermute | solution.py:21
  27.0 3.5 %collective-permute-start.5 = (bf16[2,32,512]{2,1,0:T(8,128)(2,1)S(1)}, bf16[2,32,512]{2,1,0:T(8,128)(2,1)S(1)}, u32[]{:S(2)}, u32[]{:S(2)}) collective-permute-start(bf16[2,32,512]{2,1,0:T(8,128)(2,1)S(1)} %get-tuple-element.59), channel_id=1, source_target_pairs={{0,4},{1,5},{2,6},{3,7},{4,0},{5,1},{6,2},{7,3},{8,12},{9,13},{10,... | collective-permute-start | bytes 196616 | tf_op jit(solution)/shard_map/ppermute | solution.py:21
  30.8 2.0 %collective-permute-done.15.rest_2_ = bf16[2,32,512]{2,1,0:T(8,128)(2,1)S(1)} collective-permute-done((bf16[2,32,512]{2,1,0:T(8,128)(2,1)S(1)}, bf16[2,32,512]{2,1,0:T(8,128)(2,1)S(1)}, u32[]{:S(2)}, u32[]{:S(2)}) %collective-permute-start.15) | collective-permute-done | bytes 65568 | tf_op jit(solution)/shard_map/ppermute | solution.py:21
  33.4 4.0 %collective-permute-done.5.rest_1_ = bf16[2,32,512]{2,1,0:T(8,128)(2,1)S(1)} collective-permute-done((bf16[2,32,512]{2,1,0:T(8,128)(2,1)S(1)}, bf16[2,32,512]{2,1,0:T(8,128)(2,1)S(1)}, u32[]{:S(2)}, u32[]{:S(2)}) %collective-permute-start.5) | collective-permute-done | bytes 65568 | tf_op jit(solution)/shard_map/ppermute | solution.py:21
  37.4 1.6 %collective-permute-start.7 = (bf16[8,32,512]{2,1,0:T(8,128)(2,1)S(1)}, bf16[8,32,512]{2,1,0:T(8,128)(2,1)S(1)}, u32[]{:S(2)}, u32[]{:S(2)}) collective-permute-start(bf16[8,32,512]{2,1,0:T(8,128)(2,1)S(1)} %shard_map.114.a), channel_id=1, source_target_pairs={{0,8},{8,0},{16,24},{24,16},{1,9},{9,1},{17,25},{25,17},{2,10},{10... | collective-permute-start | bytes 786440 | tf_op jit(solution)/shard_map/ppermute | solution.py:21
  39.6 1.6 %collective-permute-start.19 = (bf16[8,32,512]{2,1,0:T(8,128)(2,1)S(1)}, bf16[8,32,512]{2,1,0:T(8,128)(2,1)S(1)}, u32[]{:S(2)}, u32[]{:S(2)}) collective-permute-start(bf16[8,32,512]{2,1,0:T(8,128)(2,1)S(1)} %shard_map.118.b), channel_id=1, source_target_pairs={{0,8},{8,0},{16,24},{24,16},{1,9},{9,1},{17,25},{25,17},{2,10},{10... | collective-permute-start | bytes 786440 | tf_op jit(solution)/shard_map/ppermute | solution.py:21
  41.2 1.3 %collective-permute-start.18 = (bf16[8,32,512]{2,1,0:T(8,128)(2,1)S(1)}, bf16[8,32,512]{2,1,0:T(8,128)(2,1)S(1)}, u32[]{:S(2)}, u32[]{:S(2)}) collective-permute-start(bf16[8,32,512]{2,1,0:T(8,128)(2,1)S(1)} %shard_map.114.a), channel_id=1, source_target_pairs={{0,16},{8,24},{16,0},{24,8},{1,17},{9,25},{17,1},{25,9},{2,18},{10... | collective-permute-start | bytes 786440 | tf_op jit(solution)/shard_map/ppermute | solution.py:21
  43.0 3.7 %collective-permute-done.7.rest_0_ = bf16[8,32,512]{2,1,0:T(8,128)(2,1)S(1)} collective-permute-done((bf16[8,32,512]{2,1,0:T(8,128)(2,1)S(1)}, bf16[8,32,512]{2,1,0:T(8,128)(2,1)S(1)}, u32[]{:S(2)}, u32[]{:S(2)}) %collective-permute-start.7) | collective-permute-done | bytes 262176 | tf_op jit(solution)/shard_map/ppermute | solution.py:21
  47.3 2.0 %shard_map.119 = (bf16[4,128,512]{2,1,0:T(8,128)(2,1)S(1)}, bf16[4,512,512]{2,1,0:T(8,128)(2,1)S(1)}, f32[4,128,512]{2,1,0:T(8,128)S(1)}) custom-call(bf16[4,128,512]{2,1,0:T(8,128)(2,1)} %bitcast.19, bf16[4,512,512]{2,1,0:T(8,128)(2,1)} %bitcast.20, f32[4,128,512]{2,1,0:T(8,128)} %bitcast.15), custom_call_target="tpu_custom_call" | custom-call | flops 10000000 | bytes 1000000 | tf_op jit(solution)/shard_map/pallas_call | solution.py:37
  49.3 1.6 %shard_map.120 = (f32[4,128,512]{2,1,0:T(8,128)S(1)}, f32[4,128,512]{2,1,0:T(8,128)S(1)}) custom-call(f32[4,128,512]{2,1,0:T(8,128)} %bitcast.21, f32[4,128,512]{2,1,0:T(8,128)} %bitcast.22), custom_call_target="tpu_custom_call" | custom-call | flops 10000000 | bytes 1000000 | tf_op jit(solution)/shard_map/pallas_call | solution.py:37
  50.9 1.4 %collective-permute-done.20.lent = bf16[2,128,512]{2,1,0:T(8,128)(2,1)S(1)} collective-permute-done((bf16[2,128,512]{2,1,0:T(8,128)(2,1)S(1)}, bf16[2,128,512]{2,1,0:T(8,128)(2,1)S(1)}, u32[]{:S(2)}, u32[]{:S(2)}) %collective-permute-start.20) | collective-permute-done | bytes 262176 | tf_op jit(solution)/shard_map/ppermute | solution.py:21
  52.3 1.9 %shard_map.121 = (f32[4,128,512]{2,1,0:T(8,128)S(1)}, f32[4,128,512]{2,1,0:T(8,128)}, f32[8,128]{1,0:T(8,128)S(1)}, f32[4,128,512]{2,1,0:T(8,128)}, f32[4,128,512]{2,1,0:T(8,128)}) custom-call(s32[5]{0:T(128)S(4)} %get-tuple-element.50.meta, bf16[8,32,512]{2,1,0:T(8,128)(2,1)S(1)} %shard_map.114.a, bf16[8,32,512]{2,1,0:T(8,128)(2,1)S(1)} %shard_map.118.b, ...), custom_call_target="tpu_custom_call" | custom-call | flops 10000000 | bytes 1000000 | tf_op jit(solution)/shard_map/pallas_call | solution.py:37
  54.2 3.7 %collective-permute-done.19.rest_1_ = bf16[8,32,512]{2,1,0:T(8,128)(2,1)S(1)} collective-permute-done((bf16[8,32,512]{2,1,0:T(8,128)(2,1)S(1)}, bf16[8,32,512]{2,1,0:T(8,128)(2,1)S(1)}, u32[]{:S(2)}, u32[]{:S(2)}) %collective-permute-start.19) | collective-permute-done | bytes 262176 | tf_op jit(solution)/shard_map/ppermute | solution.py:21
  57.9 1.5 %shard_map.122 = (f32[4,128,512]{2,1,0:T(8,128)S(1)}, f32[4,128,512]{2,1,0:T(8,128)}, f32[8,128]{1,0:T(8,128)S(1)}, f32[4,128,512]{2,1,0:T(8,128)}, f32[4,128,512]{2,1,0:T(8,128)}) custom-call(s32[5]{0:T(128)S(4)} %get-tuple-element.50.meta, ...), custom_call_target="tpu_custom_call", output_to_operand_aliasing={{0}: (8, {}), {1}: (9, {}), {3}: (11, {}), {4}: (12, {})} | custom-call | flops 10000000 | bytes 1000000 | tf_op jit(solution)/shard_map/pallas_call | solution.py:37
  59.4 1.1 %shard_map.123 = (f32[4,128,512]{2,1,0:T(8,128)S(1)}, f32[4,128,512]{2,1,0:T(8,128)}, f32[8,128]{1,0:T(8,128)S(1)}) custom-call(s32[5]{0:T(128)S(4)} %get-tuple-element.50.meta, bf16[8,32,512]{2,1,0:T(8,128)(2,1)S(1)} %collective-permute-done.18.rest_0_, ...), custom_call_target="tpu_custom_call", output_to_operand_aliasing={{0}: (6, {}), {1}: (7, {})} | custom-call | flops 10000000 | bytes 1000000 | tf_op jit(solution)/shard_map/pallas_call | solution.py:37
  60.5 1.6 %collective-permute-start.21 = (f32[8,128]{1,0:T(8,128)S(1)}, f32[8,128]{1,0:T(8,128)S(1)}, u32[]{:S(2)}, u32[]{:S(2)}) collective-permute-start(f32[8,128]{1,0:T(8,128)S(1)} %get-tuple-element.86.rest_0_), channel_id=1, source_target_pairs={{0,8},{8,0},{16,24},{24,16},{1,9},{9,1},{17,25},{25,17},{2,10},{10... | collective-permute-start | bytes 12296 | tf_op jit(solution)/shard_map/ppermute | solution.py:21
  62.8 1.3 %collective-permute-start.23 = (f32[8,128]{1,0:T(8,128)S(1)}, f32[8,128]{1,0:T(8,128)S(1)}, u32[]{:S(2)}, u32[]{:S(2)}) collective-permute-start(f32[8,128]{1,0:T(8,128)S(1)} %get-tuple-element.86.rest_0_), channel_id=1, source_target_pairs={{0,24},{8,16},{16,8},{24,0},{1,25},{9,17},{17,9},{25,1},{2,26},{10... | collective-permute-start | bytes 12296 | tf_op jit(solution)/shard_map/ppermute | solution.py:21
  64.1 1.1 %shard_map.124 = (f32[4,128,512]{2,1,0:T(8,128)}, f32[4,128,512]{2,1,0:T(8,128)}) custom-call(s32[5]{0:T(128)S(4)} %get-tuple-element.50.meta, bf16[8,32,512]{2,1,0:T(8,128)(2,1)S(1)} %collective-permute-done.18.rest_0_, bf16[8,32,512]{2,1,0:T(8,128)(2,1)S(1)} %collective-permute-done.16.rest_1_, ...), custom_call_target="tpu_custom_call", output_to_operand_aliasing={{0}: (5, {}), {1}: (6, {})} | custom-call | flops 10000000 | bytes 1000000 | tf_op jit(solution)/shard_map/pallas_call | solution.py:37
  65.7 1.6 %collective-permute-done.23.rest_3_ = f32[8,128]{1,0:T(8,128)S(1)} collective-permute-done((f32[8,128]{1,0:T(8,128)S(1)}, f32[8,128]{1,0:T(8,128)S(1)}, u32[]{:S(2)}, u32[]{:S(2)}) %collective-permute-start.23) | collective-permute-done | bytes 4128 | tf_op jit(solution)/shard_map/ppermute | solution.py:21
  67.3 1.7 %shard_map.125 = (f32[4,128,512]{2,1,0:T(8,128)}, f32[4,128,512]{2,1,0:T(8,128)}, f32[4,128,512]{2,1,0:T(8,128)}, f32[4,128,512]{2,1,0:T(8,128)}) custom-call(s32[5]{0:T(128)S(4)} %get-tuple-element.50.meta, bf16[8,32,512]{2,1,0:T(8,128)(2,1)S(1)} %collective-permute-done.8.a, ...), custom_call_target="tpu_custom_call", output_to_operand_aliasing={{1}: (13, {}), {2}: (14, {}), {3}: (15, {})} | custom-call | flops 10000000 | bytes 1000000 | tf_op jit(solution)/shard_map/pallas_call | solution.py:37
  (31 shorter events, 4.7 us)
Async XLA Ops:
  4.1 9.7 %collective-permute-start.10 = (bf16[4,32,512]{2,1,0:T(8,128)(2,1)S(1)}, bf16[4,32,512]{2,1,0:T(8,128)(2,1)S(1)}, u32[]{:S(2)}, u32[]{:S(2)}) collective-permute-start(bf16[4,32,512]{2,1,0:T(8,128)(2,1)S(1)} %get-tuple-element.64), channel_id=1, source_target_pairs={{0,16},{8,24},{16,0},{24,8},{1,17},{9,25},{17,1},{25,9},{2,18},{10... | collective-permute-start | bytes 393224 | tf_op jit(solution)/shard_map/ppermute | solution.py:21
  7.2 10.1 %collective-permute-start.11 = (bf16[4,32,512]{2,1,0:T(8,128)(2,1)S(1)}, bf16[4,32,512]{2,1,0:T(8,128)(2,1)S(1)}, u32[]{:S(2)}, u32[]{:S(2)}) collective-permute-start(bf16[4,32,512]{2,1,0:T(8,128)(2,1)S(1)} %get-tuple-element.65), channel_id=1, source_target_pairs={{0,24},{8,16},{16,8},{24,0},{1,25},{9,17},{17,9},{25,1},{2,26},{10... | collective-permute-start | bytes 393224 | tf_op jit(solution)/shard_map/ppermute | solution.py:21
  8.6 8.7 %collective-permute-start.9 = (bf16[4,32,512]{2,1,0:T(8,128)(2,1)S(1)}, bf16[4,32,512]{2,1,0:T(8,128)(2,1)S(1)}, u32[]{:S(2)}, u32[]{:S(2)}) collective-permute-start(bf16[4,32,512]{2,1,0:T(8,128)(2,1)S(1)} %get-tuple-element.63), channel_id=1, source_target_pairs={{0,8},{8,0},{16,24},{24,16},{1,9},{9,1},{17,25},{25,17},{2,10},{10... | collective-permute-start | bytes 393224 | tf_op jit(solution)/shard_map/ppermute | solution.py:21
  8.7 10.0 %collective-permute-start = (bf16[4,32,512]{2,1,0:T(8,128)(2,1)S(1)}, bf16[4,32,512]{2,1,0:T(8,128)(2,1)S(1)}, u32[]{:S(2)}, u32[]{:S(2)}) collective-permute-start(bf16[4,32,512]{2,1,0:T(8,128)(2,1)S(1)} %get-tuple-element.53), channel_id=1, source_target_pairs={{0,8},{8,0},{16,24},{24,16},{1,9},{9,1},{17,25},{25,17},{2,10},{10... | collective-permute-start | bytes 393224 | tf_op jit(solution)/shard_map/ppermute | solution.py:21
  10.7 8.0 %collective-permute-start.1 = (bf16[4,32,512]{2,1,0:T(8,128)(2,1)S(1)}, bf16[4,32,512]{2,1,0:T(8,128)(2,1)S(1)}, u32[]{:S(2)}, u32[]{:S(2)}) collective-permute-start(bf16[4,32,512]{2,1,0:T(8,128)(2,1)S(1)} %get-tuple-element.54), channel_id=1, source_target_pairs={{0,16},{8,24},{16,0},{24,8},{1,17},{9,25},{17,1},{25,9},{2,18},{10... | collective-permute-start | bytes 393224 | tf_op jit(solution)/shard_map/ppermute | solution.py:21
  13.8 7.7 %collective-permute-start.2 = (bf16[4,32,512]{2,1,0:T(8,128)(2,1)S(1)}, bf16[4,32,512]{2,1,0:T(8,128)(2,1)S(1)}, u32[]{:S(2)}, u32[]{:S(2)}) collective-permute-start(bf16[4,32,512]{2,1,0:T(8,128)(2,1)S(1)} %get-tuple-element.55), channel_id=1, source_target_pairs={{0,24},{8,16},{16,8},{24,0},{1,25},{9,17},{17,9},{25,1},{2,26},{10... | collective-permute-start | bytes 393224 | tf_op jit(solution)/shard_map/ppermute | solution.py:21
  17.4 4.3 %collective-permute-start.12 = (bf16[4,32,512]{2,1,0:T(8,128)(2,1)S(1)}, bf16[4,32,512]{2,1,0:T(8,128)(2,1)S(1)}, u32[]{:S(2)}, u32[]{:S(2)}) collective-permute-start(bf16[4,32,512]{2,1,0:T(8,128)(2,1)S(1)} %get-tuple-element.67), channel_id=1, source_target_pairs={{0,1},{1,0},{2,3},{3,2},{4,5},{5,4},{6,7},{7,6},{8,9},{9,8},{10,11... | collective-permute-start | bytes 393224 | tf_op jit(solution)/shard_map/ppermute | solution.py:21
  21.6 4.6 %collective-permute-start.3 = (bf16[4,32,512]{2,1,0:T(8,128)(2,1)S(1)}, bf16[4,32,512]{2,1,0:T(8,128)(2,1)S(1)}, u32[]{:S(2)}, u32[]{:S(2)}) collective-permute-start(bf16[4,32,512]{2,1,0:T(8,128)(2,1)S(1)} %get-tuple-element.57), channel_id=1, source_target_pairs={{0,1},{1,0},{2,3},{3,2},{4,5},{5,4},{6,7},{7,6},{8,9},{9,8},{10,11... | collective-permute-start | bytes 393224 | tf_op jit(solution)/shard_map/ppermute | solution.py:21
  21.8 8.7 %collective-permute-start.13 = (bf16[2,32,512]{2,1,0:T(8,128)(2,1)S(1)}, bf16[2,32,512]{2,1,0:T(8,128)(2,1)S(1)}, u32[]{:S(2)}, u32[]{:S(2)}) collective-permute-start(bf16[2,32,512]{2,1,0:T(8,128)(2,1)S(1)} %get-tuple-element.68), channel_id=1, source_target_pairs={{0,2},{1,3},{2,0},{3,1},{4,6},{5,7},{6,4},{7,5},{8,10},{9,11},{10,... | collective-permute-start | bytes 196616 | tf_op jit(solution)/shard_map/ppermute | solution.py:21
  23.4 7.4 %collective-permute-start.14 = (bf16[2,32,512]{2,1,0:T(8,128)(2,1)S(1)}, bf16[2,32,512]{2,1,0:T(8,128)(2,1)S(1)}, u32[]{:S(2)}, u32[]{:S(2)}) collective-permute-start(bf16[2,32,512]{2,1,0:T(8,128)(2,1)S(1)} %get-tuple-element.69), channel_id=1, source_target_pairs={{0,4},{1,5},{2,6},{3,7},{4,0},{5,1},{6,2},{7,3},{8,12},{9,13},{10,... | collective-permute-start | bytes 196616 | tf_op jit(solution)/shard_map/ppermute | solution.py:21
  26.0 6.8 %collective-permute-start.15 = (bf16[2,32,512]{2,1,0:T(8,128)(2,1)S(1)}, bf16[2,32,512]{2,1,0:T(8,128)(2,1)S(1)}, u32[]{:S(2)}, u32[]{:S(2)}) collective-permute-start(bf16[2,32,512]{2,1,0:T(8,128)(2,1)S(1)} %get-tuple-element.70), channel_id=1, source_target_pairs={{0,6},{1,7},{2,4},{3,5},{4,2},{5,3},{6,0},{7,1},{8,14},{9,15},{10,... | collective-permute-start | bytes 196616 | tf_op jit(solution)/shard_map/ppermute | solution.py:21
  26.2 7.2 %collective-permute-start.4 = (bf16[2,32,512]{2,1,0:T(8,128)(2,1)S(1)}, bf16[2,32,512]{2,1,0:T(8,128)(2,1)S(1)}, u32[]{:S(2)}, u32[]{:S(2)}) collective-permute-start(bf16[2,32,512]{2,1,0:T(8,128)(2,1)S(1)} %get-tuple-element.58), channel_id=1, source_target_pairs={{0,2},{1,3},{2,0},{3,1},{4,6},{5,7},{6,4},{7,5},{8,10},{9,11},{10,... | collective-permute-start | bytes 196616 | tf_op jit(solution)/shard_map/ppermute | solution.py:21
  27.0 10.4 %collective-permute-start.5 = (bf16[2,32,512]{2,1,0:T(8,128)(2,1)S(1)}, bf16[2,32,512]{2,1,0:T(8,128)(2,1)S(1)}, u32[]{:S(2)}, u32[]{:S(2)}) collective-permute-start(bf16[2,32,512]{2,1,0:T(8,128)(2,1)S(1)} %get-tuple-element.59), channel_id=1, source_target_pairs={{0,4},{1,5},{2,6},{3,7},{4,0},{5,1},{6,2},{7,3},{8,12},{9,13},{10,... | collective-permute-start | bytes 196616 | tf_op jit(solution)/shard_map/ppermute | solution.py:21
  30.5 7.0 %collective-permute-start.6 = (bf16[2,32,512]{2,1,0:T(8,128)(2,1)S(1)}, bf16[2,32,512]{2,1,0:T(8,128)(2,1)S(1)}, u32[]{:S(2)}, u32[]{:S(2)}) collective-permute-start(bf16[2,32,512]{2,1,0:T(8,128)(2,1)S(1)} %get-tuple-element.60), channel_id=1, source_target_pairs={{0,6},{1,7},{2,4},{3,5},{4,2},{5,3},{6,0},{7,1},{8,14},{9,15},{10,... | collective-permute-start | bytes 196616 | tf_op jit(solution)/shard_map/ppermute | solution.py:21
  32.8 9.7 %collective-permute-start.16 = (bf16[8,32,512]{2,1,0:T(8,128)(2,1)S(1)}, bf16[8,32,512]{2,1,0:T(8,128)(2,1)S(1)}, u32[]{:S(2)}, u32[]{:S(2)}) collective-permute-start(bf16[8,32,512]{2,1,0:T(8,128)(2,1)S(1)} %shard_map.118.b), channel_id=1, source_target_pairs={{0,16},{8,24},{16,0},{24,8},{1,17},{9,25},{17,1},{25,9},{2,18},{10... | collective-permute-start | bytes 786440 | tf_op jit(solution)/shard_map/ppermute | solution.py:21
  37.4 9.2 %collective-permute-start.7 = (bf16[8,32,512]{2,1,0:T(8,128)(2,1)S(1)}, bf16[8,32,512]{2,1,0:T(8,128)(2,1)S(1)}, u32[]{:S(2)}, u32[]{:S(2)}) collective-permute-start(bf16[8,32,512]{2,1,0:T(8,128)(2,1)S(1)} %shard_map.114.a), channel_id=1, source_target_pairs={{0,8},{8,0},{16,24},{24,16},{1,9},{9,1},{17,25},{25,17},{2,10},{10... | collective-permute-start | bytes 786440 | tf_op jit(solution)/shard_map/ppermute | solution.py:21
  39.0 13.3 %collective-permute-start.20 = (bf16[2,128,512]{2,1,0:T(8,128)(2,1)S(1)}, bf16[2,128,512]{2,1,0:T(8,128)(2,1)S(1)}, u32[]{:S(2)}, u32[]{:S(2)}) collective-permute-start(bf16[2,128,512]{2,1,0:T(8,128)(2,1)S(1)} %get-tuple-element.76), channel_id=1, source_target_pairs={{0,24},{8,16},{16,8},{24,0},{1,25},{9,17},{17,9},{25,1},{2,26},{10... | collective-permute-start | bytes 786440 | tf_op jit(solution)/shard_map/ppermute | solution.py:21
  39.6 18.4 %collective-permute-start.19 = (bf16[8,32,512]{2,1,0:T(8,128)(2,1)S(1)}, bf16[8,32,512]{2,1,0:T(8,128)(2,1)S(1)}, u32[]{:S(2)}, u32[]{:S(2)}) collective-permute-start(bf16[8,32,512]{2,1,0:T(8,128)(2,1)S(1)} %shard_map.118.b), channel_id=1, source_target_pairs={{0,8},{8,0},{16,24},{24,16},{1,9},{9,1},{17,25},{25,17},{2,10},{10... | collective-permute-start | bytes 786440 | tf_op jit(solution)/shard_map/ppermute | solution.py:21
  41.2 18.2 %collective-permute-start.18 = (bf16[8,32,512]{2,1,0:T(8,128)(2,1)S(1)}, bf16[8,32,512]{2,1,0:T(8,128)(2,1)S(1)}, u32[]{:S(2)}, u32[]{:S(2)}) collective-permute-start(bf16[8,32,512]{2,1,0:T(8,128)(2,1)S(1)} %shard_map.114.a), channel_id=1, source_target_pairs={{0,16},{8,24},{16,0},{24,8},{1,17},{9,25},{17,1},{25,9},{2,18},{10... | collective-permute-start | bytes 786440 | tf_op jit(solution)/shard_map/ppermute | solution.py:21
  42.5 24.8 %collective-permute-start.17 = (bf16[8,32,512]{2,1,0:T(8,128)(2,1)S(1)}, bf16[8,32,512]{2,1,0:T(8,128)(2,1)S(1)}, u32[]{:S(2)}, u32[]{:S(2)}) collective-permute-start(bf16[8,32,512]{2,1,0:T(8,128)(2,1)S(1)} %collective-permute-done.16.rest_1_), channel_id=1, source_target_pairs={{0,8},{8,0},{16,24},{24,16},{1,9},{9,1},{17,25},{25,17},{2,10},{10... | collective-permute-start | bytes 786440 | tf_op jit(solution)/shard_map/ppermute | solution.py:21
  46.7 20.6 %collective-permute-start.8 = (bf16[8,32,512]{2,1,0:T(8,128)(2,1)S(1)}, bf16[8,32,512]{2,1,0:T(8,128)(2,1)S(1)}, u32[]{:S(2)}, u32[]{:S(2)}) collective-permute-start(bf16[8,32,512]{2,1,0:T(8,128)(2,1)S(1)} %collective-permute-done.7.rest_0_), channel_id=1, source_target_pairs={{0,16},{8,24},{16,0},{24,8},{1,17},{9,25},{17,1},{25,9},{2,18},{10... | collective-permute-start | bytes 786440 | tf_op jit(solution)/shard_map/ppermute | solution.py:21
  60.5 4.7 %collective-permute-start.21 = (f32[8,128]{1,0:T(8,128)S(1)}, f32[8,128]{1,0:T(8,128)S(1)}, u32[]{:S(2)}, u32[]{:S(2)}) collective-permute-start(f32[8,128]{1,0:T(8,128)S(1)} %get-tuple-element.86.rest_0_), channel_id=1, source_target_pairs={{0,8},{8,0},{16,24},{24,16},{1,9},{9,1},{17,25},{25,17},{2,10},{10... | collective-permute-start | bytes 12296 | tf_op jit(solution)/shard_map/ppermute | solution.py:21
  62.1 3.6 %collective-permute-start.22 = (f32[8,128]{1,0:T(8,128)S(1)}, f32[8,128]{1,0:T(8,128)S(1)}, u32[]{:S(2)}, u32[]{:S(2)}) collective-permute-start(f32[8,128]{1,0:T(8,128)S(1)} %get-tuple-element.86.rest_0_), channel_id=1, source_target_pairs={{0,16},{8,24},{16,0},{24,8},{1,17},{9,25},{17,1},{25,9},{2,18},{10... | collective-permute-start | bytes 12296 | tf_op jit(solution)/shard_map/ppermute | solution.py:21
  62.8 4.5 %collective-permute-start.23 = (f32[8,128]{1,0:T(8,128)S(1)}, f32[8,128]{1,0:T(8,128)S(1)}, u32[]{:S(2)}, u32[]{:S(2)}) collective-permute-start(f32[8,128]{1,0:T(8,128)S(1)} %get-tuple-element.86.rest_0_), channel_id=1, source_target_pairs={{0,24},{8,16},{16,8},{24,0},{1,25},{9,17},{17,9},{25,1},{2,26},{10... | collective-permute-start | bytes 12296 | tf_op jit(solution)/shard_map/ppermute | solution.py:21
where the time goes:
time: 69.2 us; the launch traced here: 69 us
  starting transfers between devices  31 us (45%)
  waiting for transfers between devices  22.5 us (33%)
  Pallas kernels  14.6 us (21%)
  between operations  0.79 us (1%)
    ppermute x24, starting transfers between devices, exchange(): return lax.ppermute(value, axis, [(i, i ^ distance) for i in range(size)])  31 us
    ppermute x24, waiting for transfers between devices, exchange(): return lax.ppermute(value, axis, [(i, i ^ distance) for i in range(size)])  22.5 us
    pallas_call x15, Pallas kernels, call(): pl.pallas_call(kernel, out_shape=out, in_specs=in_specs, out_specs=out_sp...  14.6 us
  transfers between devices with their start and end apart: 24, of which 10 were waited for; matrix products, arithmetic and copies ran while one was open for 0% of the time, Pallas kernels for 14%

commit v1 on v0

--- a/solution.py
+++ b/solution.py
@@ -143,24 +143,34 @@
     )
 
 
-def fetch_kernel(*refs):
+def fetch_kernel(whole, meta, *refs):
     count = len(refs) // 2
     sources, outs, sems = refs[:count], refs[count:-1], refs[-1]
-    copies = [pltpu.make_async_copy(a, b, sems.at[at]) for at, (a, b) in enumerate(zip(sources, outs))]
-    for copy in copies:
-        copy.start()
-    for copy in copies:
-        copy.wait()
-
-
-def fetch(arrays):
+    slots, held = sources[0].shape[0], meta[meta.shape[0] - 1]
+    for wait in (False, True):
+        for at, (source, out) in enumerate(zip(sources, outs)):
+            for slot in range(slots):
+                copy = pltpu.make_async_copy(source.at[slot], out.at[slot], sems.at[at * slots + slot])
+                act = copy.wait if wait else copy.start
+                if whole[at]:
+                    act()
+                else:
+                    pl.when(slot < held)(act)
+                    if wait:
+
+                        @pl.when(slot >= held)
+                        def _():
+                            out[slot] = jnp.zeros(out.shape[1:], out.dtype)
+
+
+def fetch(meta, arrays, whole):
     return call(
-        fetch_kernel,
+        functools.partial(fetch_kernel, whole),
         tuple(pltpu.VMEM(x.shape, x.dtype) for x in arrays),
-        [in_hbm(x) for x in arrays],
-        [IN_HBM] * len(arrays),
+        [in_smem(meta)] + [in_hbm(x) for x in arrays],
+        [IN_SMEM] + [IN_HBM] * len(arrays),
         (IN_VMEM,) * len(arrays),
-        [pltpu.SemaphoreType.DMA((len(arrays),))],
+        [pltpu.SemaphoreType.DMA((len(arrays) * arrays[0].shape[0],))],
     )
 
 
@@ -413,8 +423,8 @@
         for k in range(1, ways):
             parts[part].append(exchange(dealt[k], "dp", k))
     lent = exchange(lent, "dp", ways - 1)
-    first = fetch(first)
-    second = fetch(second)
+    first = fetch(meta, first, (False, False, True))
+    second = fetch(meta, second, (True, True))
     blocks = []
     for part in range(chunks):
         same, other = sort(picks, parts[part], owners)

time: 69.2 us -> 69.3 us (level)
  no operation moved by 1% of the time
where the time goes in v1:
time: 69.3 us; the launch traced here: 69 us
  starting transfers between devices  31 us (45%)
  waiting for transfers between devices  22.3 us (32%)
  Pallas kernels  14.8 us (21%)
  between operations  0.79 us (1%)
    ppermute x24, starting transfers between devices, exchange(): return lax.ppermute(value, axis, [(i, i ^ distance) for i in range(size)])  31 us
    ppermute x24, waiting for transfers between devices, exchange(): return lax.ppermute(value, axis, [(i, i ^ distance) for i in range(size)])  22.3 us
    pallas_call x15, Pallas kernels, call(): pl.pallas_call(kernel, out_shape=out, in_specs=in_specs, out_specs=out_sp...  14.8 us
  transfers between devices with their start and end apart: 24, of which 10 were waited for; matrix products, arithmetic and copies ran while one was open for 0% of the time, Pallas kernels for 14%

profile of v1, /device:TPU:0, one launch (start us, length us, event | category | flops | bytes accessed | tf_op | source)
XLA Modules:
  0.0 69.0 jit_solution(18353383805013919692)
XLA Ops:
  0.6 2.0 %shard_map.111 = (bf16[4,32,512]{2,1,0:T(8,128)(2,1)S(1)}, bf16[4,32,512]{2,1,0:T(8,128)(2,1)S(1)}, bf16[4,32,512]{2,1,0:T(8,128)(2,1)S(1)}, bf16[4,32,512]{2,1,...) custom-call(s32[4,8]{1,0:T(4,128)} %bitcast.23, s32[8]{0:T(128)} %counts.1, ...), custom_call_target="tpu_custom_call" | custom-call | flops 10000000 | bytes 1000000 | tf_op jit(solution)/shard_map/pallas_call | solution.py:37
  2.7 1.5 %shard_map.115 = (bf16[4,32,512]{2,1,0:T(8,128)(2,1)S(1)}, bf16[4,32,512]{2,1,0:T(8,128)(2,1)S(1)}, bf16[4,32,512]{2,1,0:T(8,128)(2,1)S(1)}, bf16[4,32,512]{2,1,0:T(8,128)(2,1)S(1)}, bf16[2,128,512]{2,1,0:T(8,128)(2,1)S(1)}) custom-call(s32[16]{0:T(128)S(4)} %get-tuple-element.61.order, s32[5]{0:T(128)S(4)} %get-tuple-element.50.meta, ...), custom_call_target="tpu_custom_call" | custom-call | flops 10000000 | bytes 1000000 | tf_op jit(solution)/shard_map/pallas_call | solution.py:37
  4.1 3.1 %collective-permute-start.10 = (bf16[4,32,512]{2,1,0:T(8,128)(2,1)S(1)}, bf16[4,32,512]{2,1,0:T(8,128)(2,1)S(1)}, u32[]{:S(2)}, u32[]{:S(2)}) collective-permute-start(bf16[4,32,512]{2,1,0:T(8,128)(2,1)S(1)} %get-tuple-element.64), channel_id=1, source_target_pairs={{0,16},{8,24},{16,0},{24,8},{1,17},{9,25},{17,1},{25,9},{2,18},{10... | collective-permute-start | bytes 393224 | tf_op jit(solution)/shard_map/ppermute | solution.py:21
  7.2 1.4 %collective-permute-start.11 = (bf16[4,32,512]{2,1,0:T(8,128)(2,1)S(1)}, bf16[4,32,512]{2,1,0:T(8,128)(2,1)S(1)}, u32[]{:S(2)}, u32[]{:S(2)}) collective-permute-start(bf16[4,32,512]{2,1,0:T(8,128)(2,1)S(1)} %get-tuple-element.65), channel_id=1, source_target_pairs={{0,24},{8,16},{16,8},{24,0},{1,25},{9,17},{17,9},{25,1},{2,26},{10... | collective-permute-start | bytes 393224 | tf_op jit(solution)/shard_map/ppermute | solution.py:21
  8.7 1.9 %collective-permute-start = (bf16[4,32,512]{2,1,0:T(8,128)(2,1)S(1)}, bf16[4,32,512]{2,1,0:T(8,128)(2,1)S(1)}, u32[]{:S(2)}, u32[]{:S(2)}) collective-permute-start(bf16[4,32,512]{2,1,0:T(8,128)(2,1)S(1)} %get-tuple-element.53), channel_id=1, source_target_pairs={{0,8},{8,0},{16,24},{24,16},{1,9},{9,1},{17,25},{25,17},{2,10},{10... | collective-permute-start | bytes 393224 | tf_op jit(solution)/shard_map/ppermute | solution.py:21
  10.7 1.5 %collective-permute-start.1 = (bf16[4,32,512]{2,1,0:T(8,128)(2,1)S(1)}, bf16[4,32,512]{2,1,0:T(8,128)(2,1)S(1)}, u32[]{:S(2)}, u32[]{:S(2)}) collective-permute-start(bf16[4,32,512]{2,1,0:T(8,128)(2,1)S(1)} %get-tuple-element.54), channel_id=1, source_target_pairs={{0,16},{8,24},{16,0},{24,8},{1,17},{9,25},{17,1},{25,9},{2,18},{10... | collective-permute-start | bytes 393224 | tf_op jit(solution)/shard_map/ppermute | solution.py:21
  12.2 1.7 %collective-permute-done.10.rest_2_ = bf16[4,32,512]{2,1,0:T(8,128)(2,1)S(1)} collective-permute-done((bf16[4,32,512]{2,1,0:T(8,128)(2,1)S(1)}, bf16[4,32,512]{2,1,0:T(8,128)(2,1)S(1)}, u32[]{:S(2)}, u32[]{:S(2)}) %collective-permute-start.10) | collective-permute-done | bytes 131104 | tf_op jit(solution)/shard_map/ppermute | solution.py:21
  13.8 3.5 %collective-permute-start.2 = (bf16[4,32,512]{2,1,0:T(8,128)(2,1)S(1)}, bf16[4,32,512]{2,1,0:T(8,128)(2,1)S(1)}, u32[]{:S(2)}, u32[]{:S(2)}) collective-permute-start(bf16[4,32,512]{2,1,0:T(8,128)(2,1)S(1)} %get-tuple-element.55), channel_id=1, source_target_pairs={{0,24},{8,16},{16,8},{24,0},{1,25},{9,17},{17,9},{25,1},{2,26},{10... | collective-permute-start | bytes 393224 | tf_op jit(solution)/shard_map/ppermute | solution.py:21
  17.5 1.2 %collective-permute-done.rest_1_ = bf16[4,32,512]{2,1,0:T(8,128)(2,1)S(1)} collective-permute-done((bf16[4,32,512]{2,1,0:T(8,128)(2,1)S(1)}, bf16[4,32,512]{2,1,0:T(8,128)(2,1)S(1)}, u32[]{:S(2)}, u32[]{:S(2)}) %collective-permute-start) | collective-permute-done | bytes 131104 | tf_op jit(solution)/shard_map/ppermute | solution.py:21
  18.7 2.8 %collective-permute-done.2.rest_3_ = bf16[4,32,512]{2,1,0:T(8,128)(2,1)S(1)} collective-permute-done((bf16[4,32,512]{2,1,0:T(8,128)(2,1)S(1)}, bf16[4,32,512]{2,1,0:T(8,128)(2,1)S(1)}, u32[]{:S(2)}, u32[]{:S(2)}) %collective-permute-start.2) | collective-permute-done | bytes 131104 | tf_op jit(solution)/shard_map/ppermute | solution.py:21
  21.8 1.6 %collective-permute-start.13 = (bf16[2,32,512]{2,1,0:T(8,128)(2,1)S(1)}, bf16[2,32,512]{2,1,0:T(8,128)(2,1)S(1)}, u32[]{:S(2)}, u32[]{:S(2)}) collective-permute-start(bf16[2,32,512]{2,1,0:T(8,128)(2,1)S(1)} %get-tuple-element.68), channel_id=1, source_target_pairs={{0,2},{1,3},{2,0},{3,1},{4,6},{5,7},{6,4},{7,5},{8,10},{9,11},{10,... | collective-permute-start | bytes 196616 | tf_op jit(solution)/shard_map/ppermute | solution.py:21
  23.4 2.6 %collective-permute-start.14 = (bf16[2,32,512]{2,1,0:T(8,128)(2,1)S(1)}, bf16[2,32,512]{2,1,0:T(8,128)(2,1)S(1)}, u32[]{:S(2)}, u32[]{:S(2)}) collective-permute-start(bf16[2,32,512]{2,1,0:T(8,128)(2,1)S(1)} %get-tuple-element.69), channel_id=1, source_target_pairs={{0,4},{1,5},{2,6},{3,7},{4,0},{5,1},{6,2},{7,3},{8,12},{9,13},{10,... | collective-permute-start | bytes 196616 | tf_op jit(solution)/shard_map/ppermute | solution.py:21
  26.2 0.7 %collective-permute-start.4 = (bf16[2,32,512]{2,1,0:T(8,128)(2,1)S(1)}, bf16[2,32,512]{2,1,0:T(8,128)(2,1)S(1)}, u32[]{:S(2)}, u32[]{:S(2)}) collective-permute-start(bf16[2,32,512]{2,1,0:T(8,128)(2,1)S(1)} %get-tuple-element.58), channel_id=1, source_target_pairs={{0,2},{1,3},{2,0},{3,1},{4,6},{5,7},{6,4},{7,5},{8,10},{9,11},{10,... | collective-permute-start | bytes 196616 | tf_op jit(solution)/shard_map/ppermute | solution.py:21
  27.0 3.5 %collective-permute-start.5 = (bf16[2,32,512]{2,1,0:T(8,128)(2,1)S(1)}, bf16[2,32,512]{2,1,0:T(8,128)(2,1)S(1)}, u32[]{:S(2)}, u32[]{:S(2)}) collective-permute-start(bf16[2,32,512]{2,1,0:T(8,128)(2,1)S(1)} %get-tuple-element.59), channel_id=1, source_target_pairs={{0,4},{1,5},{2,6},{3,7},{4,0},{5,1},{6,2},{7,3},{8,12},{9,13},{10,... | collective-permute-start | bytes 196616 | tf_op jit(solution)/shard_map/ppermute | solution.py:21
  30.8 2.0 %collective-permute-done.15.rest_2_ = bf16[2,32,512]{2,1,0:T(8,128)(2,1)S(1)} collective-permute-done((bf16[2,32,512]{2,1,0:T(8,128)(2,1)S(1)}, bf16[2,32,512]{2,1,0:T(8,128)(2,1)S(1)}, u32[]{:S(2)}, u32[]{:S(2)}) %collective-permute-start.15) | collective-permute-done | bytes 65568 | tf_op jit(solution)/shard_map/ppermute | solution.py:21
  33.4 4.0 %collective-permute-done.5.rest_1_ = bf16[2,32,512]{2,1,0:T(8,128)(2,1)S(1)} collective-permute-done((bf16[2,32,512]{2,1,0:T(8,128)(2,1)S(1)}, bf16[2,32,512]{2,1,0:T(8,128)(2,1)S(1)}, u32[]{:S(2)}, u32[]{:S(2)}) %collective-permute-start.5) | collective-permute-done | bytes 65568 | tf_op jit(solution)/shard_map/ppermute | solution.py:21
  37.4 1.6 %collective-permute-start.7 = (bf16[8,32,512]{2,1,0:T(8,128)(2,1)S(1)}, bf16[8,32,512]{2,1,0:T(8,128)(2,1)S(1)}, u32[]{:S(2)}, u32[]{:S(2)}) collective-permute-start(bf16[8,32,512]{2,1,0:T(8,128)(2,1)S(1)} %shard_map.114.a), channel_id=1, source_target_pairs={{0,8},{8,0},{16,24},{24,16},{1,9},{9,1},{17,25},{25,17},{2,10},{10... | collective-permute-start | bytes 786440 | tf_op jit(solution)/shard_map/ppermute | solution.py:21
  39.6 1.6 %collective-permute-start.19 = (bf16[8,32,512]{2,1,0:T(8,128)(2,1)S(1)}, bf16[8,32,512]{2,1,0:T(8,128)(2,1)S(1)}, u32[]{:S(2)}, u32[]{:S(2)}) collective-permute-start(bf16[8,32,512]{2,1,0:T(8,128)(2,1)S(1)} %shard_map.118.b), channel_id=1, source_target_pairs={{0,8},{8,0},{16,24},{24,16},{1,9},{9,1},{17,25},{25,17},{2,10},{10... | collective-permute-start | bytes 786440 | tf_op jit(solution)/shard_map/ppermute | solution.py:21
  41.2 1.3 %collective-permute-start.18 = (bf16[8,32,512]{2,1,0:T(8,128)(2,1)S(1)}, bf16[8,32,512]{2,1,0:T(8,128)(2,1)S(1)}, u32[]{:S(2)}, u32[]{:S(2)}) collective-permute-start(bf16[8,32,512]{2,1,0:T(8,128)(2,1)S(1)} %shard_map.114.a), channel_id=1, source_target_pairs={{0,16},{8,24},{16,0},{24,8},{1,17},{9,25},{17,1},{25,9},{2,18},{10... | collective-permute-start | bytes 786440 | tf_op jit(solution)/shard_map/ppermute | solution.py:21
  43.0 3.7 %collective-permute-done.7.rest_0_ = bf16[8,32,512]{2,1,0:T(8,128)(2,1)S(1)} collective-permute-done((bf16[8,32,512]{2,1,0:T(8,128)(2,1)S(1)}, bf16[8,32,512]{2,1,0:T(8,128)(2,1)S(1)}, u32[]{:S(2)}, u32[]{:S(2)}) %collective-permute-start.7) | collective-permute-done | bytes 262176 | tf_op jit(solution)/shard_map/ppermute | solution.py:21
  47.3 2.2 %shard_map.119 = (bf16[4,128,512]{2,1,0:T(8,128)(2,1)S(1)}, bf16[4,512,512]{2,1,0:T(8,128)(2,1)S(1)}, f32[4,128,512]{2,1,0:T(8,128)S(1)}) custom-call(s32[5]{0:T(128)S(4)} %get-tuple-element.50.meta, bf16[4,128,512]{2,1,0:T(8,128)(2,1)} %bitcast.20, bf16[4,512,512]{2,1,0:T(8,128)(2,1)} %bitcast.18, f32[4,128,512]{2,1,0:T(8,128)} %bitcast.17), custom_call_target="tpu_custom_call" | custom-call | flops 10000000 | bytes 1000000 | tf_op jit(solution)/shard_map/pallas_call | solution.py:37
  49.5 1.6 %shard_map.120 = (f32[4,128,512]{2,1,0:T(8,128)S(1)}, f32[4,128,512]{2,1,0:T(8,128)S(1)}) custom-call(s32[5]{0:T(128)S(4)} %get-tuple-element.50.meta, f32[4,128,512]{2,1,0:T(8,128)} %bitcast.21, f32[4,128,512]{2,1,0:T(8,128)} %bitcast.22), custom_call_target="tpu_custom_call" | custom-call | flops 10000000 | bytes 1000000 | tf_op jit(solution)/shard_map/pallas_call | solution.py:37
  51.1 1.3 %collective-permute-done.20.lent = bf16[2,128,512]{2,1,0:T(8,128)(2,1)S(1)} collective-permute-done((bf16[2,128,512]{2,1,0:T(8,128)(2,1)S(1)}, bf16[2,128,512]{2,1,0:T(8,128)(2,1)S(1)}, u32[]{:S(2)}, u32[]{:S(2)}) %collective-permute-start.20) | collective-permute-done | bytes 262176 | tf_op jit(solution)/shard_map/ppermute | solution.py:21
  52.3 1.9 %shard_map.121 = (f32[4,128,512]{2,1,0:T(8,128)S(1)}, f32[4,128,512]{2,1,0:T(8,128)}, f32[8,128]{1,0:T(8,128)S(1)}, f32[4,128,512]{2,1,0:T(8,128)}, f32[4,128,512]{2,1,0:T(8,128)}) custom-call(s32[5]{0:T(128)S(4)} %get-tuple-element.50.meta, bf16[8,32,512]{2,1,0:T(8,128)(2,1)S(1)} %shard_map.114.a, bf16[8,32,512]{2,1,0:T(8,128)(2,1)S(1)} %shard_map.118.b, ...), custom_call_target="tpu_custom_call" | custom-call | flops 10000000 | bytes 1000000 | tf_op jit(solution)/shard_map/pallas_call | solution.py:37
  54.2 3.7 %collective-permute-done.19.rest_1_ = bf16[8,32,512]{2,1,0:T(8,128)(2,1)S(1)} collective-permute-done((bf16[8,32,512]{2,1,0:T(8,128)(2,1)S(1)}, bf16[8,32,512]{2,1,0:T(8,128)(2,1)S(1)}, u32[]{:S(2)}, u32[]{:S(2)}) %collective-permute-start.19) | collective-permute-done | bytes 262176 | tf_op jit(solution)/shard_map/ppermute | solution.py:21
  57.9 1.5 %shard_map.122 = (f32[4,128,512]{2,1,0:T(8,128)S(1)}, f32[4,128,512]{2,1,0:T(8,128)}, f32[8,128]{1,0:T(8,128)S(1)}, f32[4,128,512]{2,1,0:T(8,128)}, f32[4,128,512]{2,1,0:T(8,128)}) custom-call(s32[5]{0:T(128)S(4)} %get-tuple-element.50.meta, ...), custom_call_target="tpu_custom_call", output_to_operand_aliasing={{0}: (8, {}), {1}: (9, {}), {3}: (11, {}), {4}: (12, {})} | custom-call | flops 10000000 | bytes 1000000 | tf_op jit(solution)/shard_map/pallas_call | solution.py:37
  59.4 1.1 %shard_map.123 = (f32[4,128,512]{2,1,0:T(8,128)S(1)}, f32[4,128,512]{2,1,0:T(8,128)}, f32[8,128]{1,0:T(8,128)S(1)}) custom-call(s32[5]{0:T(128)S(4)} %get-tuple-element.50.meta, bf16[8,32,512]{2,1,0:T(8,128)(2,1)S(1)} %collective-permute-done.18.rest_0_, ...), custom_call_target="tpu_custom_call", output_to_operand_aliasing={{0}: (6, {}), {1}: (7, {})} | custom-call | flops 10000000 | bytes 1000000 | tf_op jit(solution)/shard_map/pallas_call | solution.py:37
  60.5 1.6 %collective-permute-start.21 = (f32[8,128]{1,0:T(8,128)S(1)}, f32[8,128]{1,0:T(8,128)S(1)}, u32[]{:S(2)}, u32[]{:S(2)}) collective-permute-start(f32[8,128]{1,0:T(8,128)S(1)} %get-tuple-element.86.rest_0_), channel_id=1, source_target_pairs={{0,8},{8,0},{16,24},{24,16},{1,9},{9,1},{17,25},{25,17},{2,10},{10... | collective-permute-start | bytes 12296 | tf_op jit(solution)/shard_map/ppermute | solution.py:21
  62.8 1.3 %collective-permute-start.23 = (f32[8,128]{1,0:T(8,128)S(1)}, f32[8,128]{1,0:T(8,128)S(1)}, u32[]{:S(2)}, u32[]{:S(2)}) collective-permute-start(f32[8,128]{1,0:T(8,128)S(1)} %get-tuple-element.86.rest_0_), channel_id=1, source_target_pairs={{0,24},{8,16},{16,8},{24,0},{1,25},{9,17},{17,9},{25,1},{2,26},{10... | collective-permute-start | bytes 12296 | tf_op jit(solution)/shard_map/ppermute | solution.py:21
  64.1 1.1 %shard_map.124 = (f32[4,128,512]{2,1,0:T(8,128)}, f32[4,128,512]{2,1,0:T(8,128)}) custom-call(s32[5]{0:T(128)S(4)} %get-tuple-element.50.meta, bf16[8,32,512]{2,1,0:T(8,128)(2,1)S(1)} %collective-permute-done.18.rest_0_, bf16[8,32,512]{2,1,0:T(8,128)(2,1)S(1)} %collective-permute-done.16.rest_1_, ...), custom_call_target="tpu_custom_call", output_to_operand_aliasing={{0}: (5, {}), {1}: (6, {})} | custom-call | flops 10000000 | bytes 1000000 | tf_op jit(solution)/shard_map/pallas_call | solution.py:37
  65.7 1.6 %collective-permute-done.23.rest_3_ = f32[8,128]{1,0:T(8,128)S(1)} collective-permute-done((f32[8,128]{1,0:T(8,128)S(1)}, f32[8,128]{1,0:T(8,128)S(1)}, u32[]{:S(2)}, u32[]{:S(2)}) %collective-permute-start.23) | collective-permute-done | bytes 4128 | tf_op jit(solution)/shard_map/ppermute | solution.py:21
  67.3 1.7 %shard_map.125 = (f32[4,128,512]{2,1,0:T(8,128)}, f32[4,128,512]{2,1,0:T(8,128)}, f32[4,128,512]{2,1,0:T(8,128)}, f32[4,128,512]{2,1,0:T(8,128)}) custom-call(s32[5]{0:T(128)S(4)} %get-tuple-element.50.meta, bf16[8,32,512]{2,1,0:T(8,128)(2,1)S(1)} %collective-permute-done.8.a, ...), custom_call_target="tpu_custom_call", output_to_operand_aliasing={{1}: (13, {}), {2}: (14, {}), {3}: (15, {})} | custom-call | flops 10000000 | bytes 1000000 | tf_op jit(solution)/shard_map/pallas_call | solution.py:37
  (31 shorter events, 4.7 us)
Async XLA Ops:
  4.1 9.7 %collective-permute-start.10 = (bf16[4,32,512]{2,1,0:T(8,128)(2,1)S(1)}, bf16[4,32,512]{2,1,0:T(8,128)(2,1)S(1)}, u32[]{:S(2)}, u32[]{:S(2)}) collective-permute-start(bf16[4,32,512]{2,1,0:T(8,128)(2,1)S(1)} %get-tuple-element.64), channel_id=1, source_target_pairs={{0,16},{8,24},{16,0},{24,8},{1,17},{9,25},{17,1},{25,9},{2,18},{10... | collective-permute-start | bytes 393224 | tf_op jit(solution)/shard_map/ppermute | solution.py:21
  7.2 10.1 %collective-permute-start.11 = (bf16[4,32,512]{2,1,0:T(8,128)(2,1)S(1)}, bf16[4,32,512]{2,1,0:T(8,128)(2,1)S(1)}, u32[]{:S(2)}, u32[]{:S(2)}) collective-permute-start(bf16[4,32,512]{2,1,0:T(8,128)(2,1)S(1)} %get-tuple-element.65), channel_id=1, source_target_pairs={{0,24},{8,16},{16,8},{24,0},{1,25},{9,17},{17,9},{25,1},{2,26},{10... | collective-permute-start | bytes 393224 | tf_op jit(solution)/shard_map/ppermute | solution.py:21
  8.6 8.7 %collective-permute-start.9 = (bf16[4,32,512]{2,1,0:T(8,128)(2,1)S(1)}, bf16[4,32,512]{2,1,0:T(8,128)(2,1)S(1)}, u32[]{:S(2)}, u32[]{:S(2)}) collective-permute-start(bf16[4,32,512]{2,1,0:T(8,128)(2,1)S(1)} %get-tuple-element.63), channel_id=1, source_target_pairs={{0,8},{8,0},{16,24},{24,16},{1,9},{9,1},{17,25},{25,17},{2,10},{10... | collective-permute-start | bytes 393224 | tf_op jit(solution)/shard_map/ppermute | solution.py:21
  8.7 10.0 %collective-permute-start = (bf16[4,32,512]{2,1,0:T(8,128)(2,1)S(1)}, bf16[4,32,512]{2,1,0:T(8,128)(2,1)S(1)}, u32[]{:S(2)}, u32[]{:S(2)}) collective-permute-start(bf16[4,32,512]{2,1,0:T(8,128)(2,1)S(1)} %get-tuple-element.53), channel_id=1, source_target_pairs={{0,8},{8,0},{16,24},{24,16},{1,9},{9,1},{17,25},{25,17},{2,10},{10... | collective-permute-start | bytes 393224 | tf_op jit(solution)/shard_map/ppermute | solution.py:21
  10.7 8.0 %collective-permute-start.1 = (bf16[4,32,512]{2,1,0:T(8,128)(2,1)S(1)}, bf16[4,32,512]{2,1,0:T(8,128)(2,1)S(1)}, u32[]{:S(2)}, u32[]{:S(2)}) collective-permute-start(bf16[4,32,512]{2,1,0:T(8,128)(2,1)S(1)} %get-tuple-element.54), channel_id=1, source_target_pairs={{0,16},{8,24},{16,0},{24,8},{1,17},{9,25},{17,1},{25,9},{2,18},{10... | collective-permute-start | bytes 393224 | tf_op jit(solution)/shard_map/ppermute | solution.py:21
  13.8 7.7 %collective-permute-start.2 = (bf16[4,32,512]{2,1,0:T(8,128)(2,1)S(1)}, bf16[4,32,512]{2,1,0:T(8,128)(2,1)S(1)}, u32[]{:S(2)}, u32[]{:S(2)}) collective-permute-start(bf16[4,32,512]{2,1,0:T(8,128)(2,1)S(1)} %get-tuple-element.55), channel_id=1, source_target_pairs={{0,24},{8,16},{16,8},{24,0},{1,25},{9,17},{17,9},{25,1},{2,26},{10... | collective-permute-start | bytes 393224 | tf_op jit(solution)/shard_map/ppermute | solution.py:21
  17.4 4.3 %collective-permute-start.12 = (bf16[4,32,512]{2,1,0:T(8,128)(2,1)S(1)}, bf16[4,32,512]{2,1,0:T(8,128)(2,1)S(1)}, u32[]{:S(2)}, u32[]{:S(2)}) collective-permute-start(bf16[4,32,512]{2,1,0:T(8,128)(2,1)S(1)} %get-tuple-element.67), channel_id=1, source_target_pairs={{0,1},{1,0},{2,3},{3,2},{4,5},{5,4},{6,7},{7,6},{8,9},{9,8},{10,11... | collective-permute-start | bytes 393224 | tf_op jit(solution)/shard_map/ppermute | solution.py:21
  21.6 4.6 %collective-permute-start.3 = (bf16[4,32,512]{2,1,0:T(8,128)(2,1)S(1)}, bf16[4,32,512]{2,1,0:T(8,128)(2,1)S(1)}, u32[]{:S(2)}, u32[]{:S(2)}) collective-permute-start(bf16[4,32,512]{2,1,0:T(8,128)(2,1)S(1)} %get-tuple-element.57), channel_id=1, source_target_pairs={{0,1},{1,0},{2,3},{3,2},{4,5},{5,4},{6,7},{7,6},{8,9},{9,8},{10,11... | collective-permute-start | bytes 393224 | tf_op jit(solution)/shard_map/ppermute | solution.py:21
  21.8 8.7 %collective-permute-start.13 = (bf16[2,32,512]{2,1,0:T(8,128)(2,1)S(1)}, bf16[2,32,512]{2,1,0:T(8,128)(2,1)S(1)}, u32[]{:S(2)}, u32[]{:S(2)}) collective-permute-start(bf16[2,32,512]{2,1,0:T(8,128)(2,1)S(1)} %get-tuple-element.68), channel_id=1, source_target_pairs={{0,2},{1,3},{2,0},{3,1},{4,6},{5,7},{6,4},{7,5},{8,10},{9,11},{10,... | collective-permute-start | bytes 196616 | tf_op jit(solution)/shard_map/ppermute | solution.py:21
  23.4 7.4 %collective-permute-start.14 = (bf16[2,32,512]{2,1,0:T(8,128)(2,1)S(1)}, bf16[2,32,512]{2,1,0:T(8,128)(2,1)S(1)}, u32[]{:S(2)}, u32[]{:S(2)}) collective-permute-start(bf16[2,32,512]{2,1,0:T(8,128)(2,1)S(1)} %get-tuple-element.69), channel_id=1, source_target_pairs={{0,4},{1,5},{2,6},{3,7},{4,0},{5,1},{6,2},{7,3},{8,12},{9,13},{10,... | collective-permute-start | bytes 196616 | tf_op jit(solution)/shard_map/ppermute | solution.py:21
  26.0 6.8 %collective-permute-start.15 = (bf16[2,32,512]{2,1,0:T(8,128)(2,1)S(1)}, bf16[2,32,512]{2,1,0:T(8,128)(2,1)S(1)}, u32[]{:S(2)}, u32[]{:S(2)}) collective-permute-start(bf16[2,32,512]{2,1,0:T(8,128)(2,1)S(1)} %get-tuple-element.70), channel_id=1, source_target_pairs={{0,6},{1,7},{2,4},{3,5},{4,2},{5,3},{6,0},{7,1},{8,14},{9,15},{10,... | collective-permute-start | bytes 196616 | tf_op jit(solution)/shard_map/ppermute | solution.py:21
  26.2 7.2 %collective-permute-start.4 = (bf16[2,32,512]{2,1,0:T(8,128)(2,1)S(1)}, bf16[2,32,512]{2,1,0:T(8,128)(2,1)S(1)}, u32[]{:S(2)}, u32[]{:S(2)}) collective-permute-start(bf16[2,32,512]{2,1,0:T(8,128)(2,1)S(1)} %get-tuple-element.58), channel_id=1, source_target_pairs={{0,2},{1,3},{2,0},{3,1},{4,6},{5,7},{6,4},{7,5},{8,10},{9,11},{10,... | collective-permute-start | bytes 196616 | tf_op jit(solution)/shard_map/ppermute | solution.py:21
  27.0 10.4 %collective-permute-start.5 = (bf16[2,32,512]{2,1,0:T(8,128)(2,1)S(1)}, bf16[2,32,512]{2,1,0:T(8,128)(2,1)S(1)}, u32[]{:S(2)}, u32[]{:S(2)}) collective-permute-start(bf16[2,32,512]{2,1,0:T(8,128)(2,1)S(1)} %get-tuple-element.59), channel_id=1, source_target_pairs={{0,4},{1,5},{2,6},{3,7},{4,0},{5,1},{6,2},{7,3},{8,12},{9,13},{10,... | collective-permute-start | bytes 196616 | tf_op jit(solution)/shard_map/ppermute | solution.py:21
  30.5 7.0 %collective-permute-start.6 = (bf16[2,32,512]{2,1,0:T(8,128)(2,1)S(1)}, bf16[2,32,512]{2,1,0:T(8,128)(2,1)S(1)}, u32[]{:S(2)}, u32[]{:S(2)}) collective-permute-start(bf16[2,32,512]{2,1,0:T(8,128)(2,1)S(1)} %get-tuple-element.60), channel_id=1, source_target_pairs={{0,6},{1,7},{2,4},{3,5},{4,2},{5,3},{6,0},{7,1},{8,14},{9,15},{10,... | collective-permute-start | bytes 196616 | tf_op jit(solution)/shard_map/ppermute | solution.py:21
  32.8 9.7 %collective-permute-start.16 = (bf16[8,32,512]{2,1,0:T(8,128)(2,1)S(1)}, bf16[8,32,512]{2,1,0:T(8,128)(2,1)S(1)}, u32[]{:S(2)}, u32[]{:S(2)}) collective-permute-start(bf16[8,32,512]{2,1,0:T(8,128)(2,1)S(1)} %shard_map.118.b), channel_id=1, source_target_pairs={{0,16},{8,24},{16,0},{24,8},{1,17},{9,25},{17,1},{25,9},{2,18},{10... | collective-permute-start | bytes 786440 | tf_op jit(solution)/shard_map/ppermute | solution.py:21
  37.4 9.2 %collective-permute-start.7 = (bf16[8,32,512]{2,1,0:T(8,128)(2,1)S(1)}, bf16[8,32,512]{2,1,0:T(8,128)(2,1)S(1)}, u32[]{:S(2)}, u32[]{:S(2)}) collective-permute-start(bf16[8,32,512]{2,1,0:T(8,128)(2,1)S(1)} %shard_map.114.a), channel_id=1, source_target_pairs={{0,8},{8,0},{16,24},{24,16},{1,9},{9,1},{17,25},{25,17},{2,10},{10... | collective-permute-start | bytes 786440 | tf_op jit(solution)/shard_map/ppermute | solution.py:21
  39.0 13.3 %collective-permute-start.20 = (bf16[2,128,512]{2,1,0:T(8,128)(2,1)S(1)}, bf16[2,128,512]{2,1,0:T(8,128)(2,1)S(1)}, u32[]{:S(2)}, u32[]{:S(2)}) collective-permute-start(bf16[2,128,512]{2,1,0:T(8,128)(2,1)S(1)} %get-tuple-element.76), channel_id=1, source_target_pairs={{0,24},{8,16},{16,8},{24,0},{1,25},{9,17},{17,9},{25,1},{2,26},{10... | collective-permute-start | bytes 786440 | tf_op jit(solution)/shard_map/ppermute | solution.py:21
  39.6 18.4 %collective-permute-start.19 = (bf16[8,32,512]{2,1,0:T(8,128)(2,1)S(1)}, bf16[8,32,512]{2,1,0:T(8,128)(2,1)S(1)}, u32[]{:S(2)}, u32[]{:S(2)}) collective-permute-start(bf16[8,32,512]{2,1,0:T(8,128)(2,1)S(1)} %shard_map.118.b), channel_id=1, source_target_pairs={{0,8},{8,0},{16,24},{24,16},{1,9},{9,1},{17,25},{25,17},{2,10},{10... | collective-permute-start | bytes 786440 | tf_op jit(solution)/shard_map/ppermute | solution.py:21
  41.2 18.2 %collective-permute-start.18 = (bf16[8,32,512]{2,1,0:T(8,128)(2,1)S(1)}, bf16[8,32,512]{2,1,0:T(8,128)(2,1)S(1)}, u32[]{:S(2)}, u32[]{:S(2)}) collective-permute-start(bf16[8,32,512]{2,1,0:T(8,128)(2,1)S(1)} %shard_map.114.a), channel_id=1, source_target_pairs={{0,16},{8,24},{16,0},{24,8},{1,17},{9,25},{17,1},{25,9},{2,18},{10... | collective-permute-start | bytes 786440 | tf_op jit(solution)/shard_map/ppermute | solution.py:21
  42.5 24.8 %collective-permute-start.17 = (bf16[8,32,512]{2,1,0:T(8,128)(2,1)S(1)}, bf16[8,32,512]{2,1,0:T(8,128)(2,1)S(1)}, u32[]{:S(2)}, u32[]{:S(2)}) collective-permute-start(bf16[8,32,512]{2,1,0:T(8,128)(2,1)S(1)} %collective-permute-done.16.rest_1_), channel_id=1, source_target_pairs={{0,8},{8,0},{16,24},{24,16},{1,9},{9,1},{17,25},{25,17},{2,10},{10... | collective-permute-start | bytes 786440 | tf_op jit(solution)/shard_map/ppermute | solution.py:21
  46.7 20.6 %collective-permute-start.8 = (bf16[8,32,512]{2,1,0:T(8,128)(2,1)S(1)}, bf16[8,32,512]{2,1,0:T(8,128)(2,1)S(1)}, u32[]{:S(2)}, u32[]{:S(2)}) collective-permute-start(bf16[8,32,512]{2,1,0:T(8,128)(2,1)S(1)} %collective-permute-done.7.rest_0_), channel_id=1, source_target_pairs={{0,16},{8,24},{16,0},{24,8},{1,17},{9,25},{17,1},{25,9},{2,18},{10... | collective-permute-start | bytes 786440 | tf_op jit(solution)/shard_map/ppermute | solution.py:21
  60.5 4.7 %collective-permute-start.21 = (f32[8,128]{1,0:T(8,128)S(1)}, f32[8,128]{1,0:T(8,128)S(1)}, u32[]{:S(2)}, u32[]{:S(2)}) collective-permute-start(f32[8,128]{1,0:T(8,128)S(1)} %get-tuple-element.86.rest_0_), channel_id=1, source_target_pairs={{0,8},{8,0},{16,24},{24,16},{1,9},{9,1},{17,25},{25,17},{2,10},{10... | collective-permute-start | bytes 12296 | tf_op jit(solution)/shard_map/ppermute | solution.py:21
  62.1 3.6 %collective-permute-start.22 = (f32[8,128]{1,0:T(8,128)S(1)}, f32[8,128]{1,0:T(8,128)S(1)}, u32[]{:S(2)}, u32[]{:S(2)}) collective-permute-start(f32[8,128]{1,0:T(8,128)S(1)} %get-tuple-element.86.rest_0_), channel_id=1, source_target_pairs={{0,16},{8,24},{16,0},{24,8},{1,17},{9,25},{17,1},{25,9},{2,18},{10... | collective-permute-start | bytes 12296 | tf_op jit(solution)/shard_map/ppermute | solution.py:21
  62.8 4.5 %collective-permute-start.23 = (f32[8,128]{1,0:T(8,128)S(1)}, f32[8,128]{1,0:T(8,128)S(1)}, u32[]{:S(2)}, u32[]{:S(2)}) collective-permute-start(f32[8,128]{1,0:T(8,128)S(1)} %get-tuple-element.86.rest_0_), channel_id=1, source_target_pairs={{0,24},{8,16},{16,8},{24,0},{1,25},{9,17},{17,9},{25,1},{2,26},{10... | collective-permute-start | bytes 12296 | tf_op jit(solution)/shard_map/ppermute | solution.py:21
